TPU v7x, 32 devices: a whole 2x2x4 slice. The times are simulated.
32 devices in a mesh: gx: 4 (over y, x), gy: 2 (over core), gz: 4 (over z).
Axes of the slice: x: 2, y: 2, z: 4, core: 2. Of those that a mesh axis runs over, the one named last changes fastest.
Arguments:
- pair_blocks: float32 [529, 1024], P(None, ('gx', 'gy', 'gz')), may hold values from -6 to 6
- basis_map: float32 [529, 64], replicated, may hold values from -0.25 to 0.25
- pair_cells: int32 [3, 1024], P(None, ('gx', 'gy', 'gz')), may hold values from 0 to 511, as said below
- pair_offsets: float32 [3, 1024], P(None, ('gx', 'gy', 'gz')), may hold values from 0 to 1
- exponent_index: int32 [1024], P(('gx', 'gy', 'gz')), may hold values from 0 to 15
- radius_index: int32 [1024], P(('gx', 'gy', 'gz')), may hold values from 0 to 4
- exponents: float32 [16], replicated, may hold values from 7 to 9
Outputs:
- density: float32 [32, 64, 512], P('gx', 'gy', 'gz')
- spectrum: float32 [2, 512, 64, 32], P(None, ('gy', 'gz'), 'gx')
Inputs may be any that keep to these rules, and one draw needn't show every extreme that they name: The y of pair_cells column p lies among the 32 cells, and its z among the 128 cells, of the gy and gz index of the device that holds column p. Of the pairs that one device holds at most 16 have x in the same run of 8 cells that one gx index holds, and in every draw some such run gets exactly 16 from every device.
All inputs are finite; a program needn't handle non-finite values.
Results may differ from a plain program's by a relative error of at most 0.0003.
Values sent between devices are 32-bit elements; how exact they have to be, the bound alone decides.
A program may use at most 64 MiB of HBM per device.

v0:
```python
import math

import jax
import jax.numpy as jnp
from jax import lax
from jax.sharding import PartitionSpec as P

DEG = 3
HALO = 8
CX = 8
CY = 32
CZ = 128


highest = lax.Precision.HIGHEST


def padded_2(block, sides, width):
    for axis, dim in sides:
        count = lax.axis_size(axis)
        forward = [(i, i + 1) for i in range(count - 1)]
        forward.append((count - 1, 0))
        backward = [(target, source) for source, target in forward]
        low = lax.ppermute(
            lax.slice_in_dim(block, block.shape[dim] - width, None, axis=dim), axis, forward
        )
        high = lax.ppermute(lax.slice_in_dim(block, 0, width, axis=dim), axis, backward)
        block = jnp.concatenate([low, block, high], axis=dim)
    return block


def place_columns(values, slot_ids, slot_count):
    empty = jnp.zeros((values.shape[0], slot_count), values.dtype)
    return empty.at[:, slot_ids].set(values)


def axis_factors(centres, offsets_row, exponent_values, radius_cells, anchor, extent):
    coordinate = anchor - HALO + jnp.arange(extent, dtype=jnp.int32)
    offset_cells = coordinate[None, :] - centres[:, None]
    distance = offset_cells.astype(jnp.float32) - offsets_row[:, None]
    inside = (jnp.abs(offset_cells) <= radius_cells[:, None]).astype(jnp.float32)
    envelope = jnp.exp(-exponent_values[:, None] * distance * distance) * inside
    scaled = distance / HALO
    return jnp.stack([scaled**degree * envelope for degree in range(DEG + 1)], 1)


def add_along(target, start, piece, along_dim):
    index = [slice(None)] * target.ndim
    index[along_dim] = slice(start, start + piece.shape[along_dim])
    return target.at[tuple(index)].add(piece)


def fold_rims(padded, along_dim, interior):
    lower_rim = lax.slice_in_dim(padded, 0, HALO, axis=along_dim)
    middle = lax.slice_in_dim(padded, 2 * HALO, 2 * HALO + interior, axis=along_dim)
    upper_rim = lax.slice_in_dim(padded, interior + 3 * HALO, interior + 4 * HALO, axis=along_dim)
    middle = add_along(middle, 0, lower_rim, along_dim)
    return add_along(middle, interior - HALO, upper_rim, along_dim)


def dft_parts(length):
    indices = jnp.arange(length, dtype=jnp.int32)
    product = indices[:, None] * indices[None, :] % length
    angles = product.astype(jnp.float32) * (2.0 * math.pi / length)
    factor = 1.0 / math.sqrt(length)
    return (jnp.cos(angles) * factor, jnp.sin(angles) * factor)


def shards(
    pair_blocks, basis_map, pair_cells, pair_offsets, exponent_index, radius_index, exponents
):
    pair_dev = pair_blocks.shape[1]
    x_devices = lax.axis_size("gx")
    capacity = 2 * pair_dev // x_devices
    slot_count = x_devices * capacity
    selector = (
        exponent_index[None, :] == jnp.arange(exponents.shape[0], dtype=jnp.int32)[:, None]
    ).astype(jnp.float32)
    radius_own = HALO - radius_index
    radius_float = radius_own.astype(jnp.float32)
    exponent_values = jnp.dot(exponents, selector, precision=highest) / (
        radius_float * radius_float
    )
    owners = pair_cells[0] // CX
    member = (owners[:, None] == jnp.arange(x_devices, dtype=jnp.int32)[None, :]).astype(jnp.int32)
    within = jnp.sum((jnp.cumsum(member, axis=0) - member) * member, axis=1)
    slot_ids = owners * capacity + within
    extras = jnp.concatenate([pair_offsets, exponent_values[None, :]], 0)
    labels = jnp.concatenate([pair_cells, radius_own[None, :]], 0)
    routed_labels = place_columns(labels, slot_ids, slot_count).reshape(4, x_devices, capacity)
    outgoing = place_columns(jnp.concatenate([pair_blocks, extras], 0), slot_ids, slot_count)
    arrived, arrived_labels = (
        lax.all_to_all(
            outgoing.reshape(-1, x_devices, capacity), "gx", split_axis=1, concat_axis=1, tiled=True
        ),
        lax.all_to_all(routed_labels, "gx", split_axis=1, concat_axis=1, tiled=True),
    )
    arrived = arrived.reshape(-1, slot_count)
    pair_coefs = jnp.dot(basis_map.T, arrived[:-4], precision=highest)
    arrived_labels = arrived_labels.reshape(4, slot_count)
    offsets_in = arrived[-4:-1]
    exponent_in = arrived[-1]
    centres = arrived_labels[:3]
    radius_cells = arrived_labels[3]
    extent_x = CX + 2 * HALO
    extent_y = CY + 2 * HALO
    extent_z = CZ + 2 * HALO
    along_x = axis_factors(
        centres[0], offsets_in[0], exponent_in, radius_cells, lax.axis_index("gx") * CX, extent_x
    )
    along_y = axis_factors(
        centres[1], offsets_in[1], exponent_in, radius_cells, lax.axis_index("gy") * CY, extent_y
    )
    along_z = axis_factors(
        centres[2], offsets_in[2], exponent_in, radius_cells, lax.axis_index("gz") * CZ, extent_z
    )
    side = DEG + 1
    coef_cube = pair_coefs.T.reshape(slot_count, side, side, side)
    partial_z = jnp.einsum("sijk,skc->sijc", coef_cube, along_z, precision=highest)
    plane_groups = jnp.transpose(along_x.reshape(slot_count, side, extent_x // 8, 8), (2, 0, 1, 3))

    def planes(group_x):
        mixed_planes = jnp.einsum("sia,sijc->sjac", group_x, partial_z, precision=highest)
        return jnp.einsum("sjb,sjac->abc", along_y, mixed_planes, precision=highest)

    extended = lax.map(planes, plane_groups).reshape(extent_x, extent_y, extent_z)
    padded = padded_2(extended, (("gx", 0), ("gy", 1), ("gz", 2)), HALO)
    density = fold_rims(fold_rims(fold_rims(padded, 0, CX), 1, CY), 2, CZ)
    depth_local = lax.all_to_all(density, "gz", split_axis=1, concat_axis=2, tiled=True)
    depth_size = depth_local.shape[2]
    cosine_z, sine_z = dft_parts(depth_size)
    real_z = jnp.einsum("xyz,zk->xyk", depth_local, cosine_z, precision=highest)
    imag_z = -jnp.einsum("xyz,zk->xyk", depth_local, sine_z, precision=highest)
    section_z = jnp.stack([real_z, imag_z])
    rows_devices = lax.axis_size("gy")
    depth_devices = lax.axis_size("gz")
    depth_piece = depth_size // (rows_devices * depth_devices)
    split_view = section_z.reshape(
        2, CX, 1, 1, section_z.shape[2], rows_devices, depth_devices, depth_piece
    )
    moved_rows = lax.all_to_all(
        lax.all_to_all(split_view, "gy", split_axis=5, concat_axis=2, tiled=True),
        "gz",
        split_axis=6,
        concat_axis=3,
        tiled=True,
    )
    rows_local = moved_rows.reshape(2, CX, -1, depth_piece)
    cosine_y, sine_y = dft_parts(rows_local.shape[2])
    real_in = rows_local[0]
    imag_in = rows_local[1]
    real_y = jnp.einsum("xyk,yl->klx", real_in, cosine_y, precision=highest) + jnp.einsum(
        "xyk,yl->klx", imag_in, sine_y, precision=highest
    )
    imag_y = jnp.einsum("xyk,yl->klx", imag_in, cosine_y, precision=highest) - jnp.einsum(
        "xyk,yl->klx", real_in, sine_y, precision=highest
    )
    section_y = jnp.stack([real_y, imag_y])
    width_local = lax.all_to_all(section_y, "gx", split_axis=2, concat_axis=3, tiled=True)
    cosine_x, sine_x = dft_parts(width_local.shape[3])
    real_w = width_local[0]
    imag_w = width_local[1]
    real_x = jnp.einsum("kyx,xm->kym", real_w, cosine_x, precision=highest) + jnp.einsum(
        "kyx,xm->kym", imag_w, sine_x, precision=highest
    )
    imag_x = jnp.einsum("kyx,xm->kym", imag_w, cosine_x, precision=highest) - jnp.einsum(
        "kyx,xm->kym", real_w, sine_x, precision=highest
    )
    spectrum = jnp.stack([real_x, imag_x])
    return (density, spectrum)


def solution(mesh):
    placed = (
        P(None, ("gx", "gy", "gz")),
        P(),
        P(None, ("gx", "gy", "gz")),
        P(None, ("gx", "gy", "gz")),
        P(("gx", "gy", "gz")),
        P(("gx", "gy", "gz")),
        P(),
    )
    return jax.shard_map(
        shards,
        mesh=mesh,
        in_specs=placed,
        out_specs=(P("gx", "gy", "gz"), P(None, ("gy", "gz"), "gx", None)),
        check_vma=False,
    )
```

profile of v0, /device:TPU:0, one launch (start us, length us, event | category | flops | bytes accessed | tf_op | source)
XLA Modules:
  0.0 139.2 jit_solution(2050929000422461326)
XLA Ops:
  5.2 5.2 %all-to-all-start = ((s32[4,4,16]{2,0,1:T(4,128)}), s32[4,4,16]{2,0,1:T(4,128)S(1)}, u32[]{:S(2)}, u32[]{:S(2)}) async-start(s32[4,4,16]{2,0,1:T(4,128)} %copy.77), calls=%async_computation | async-start | bytes 16384 | tf_op jit(solution)/shard_map/all_to_all | solution.py:96
  15.1 3.9 %all-to-all-start.1 = ((f32[533,4,16]{0,2,1:T(8,128)}), f32[533,4,16]{0,2,1:T(8,128)S(1)}, u32[]{:S(2)}, u32[]{:S(2)}) async-start(f32[533,4,16]{0,2,1:T(8,128)} %bitcast.20), calls=%async_computation.1 | async-start | bytes 327680 | tf_op jit(solution)/shard_map/all_to_all | solution.py:93
  19.3 4.7 %all-to-all-done.1 = f32[533,4,16]{0,2,1:T(8,128)S(1)} async-done(((f32[533,4,16]{0,2,1:T(8,128)}), f32[533,4,16]{0,2,1:T(8,128)S(1)}, u32[]{:S(2)}, u32[]{:S(2)}) %all-to-all-start.1) | async-done | bytes 136480 | tf_op jit(solution)/shard_map/all_to_all | solution.py:93
  27.4 15.3 %while.18 = (s32[]{:T(128)}, f32[3,8,48,144]{3,2,1,0:T(8,128)S(1)}, f32[3,64,4,8]{1,3,0,2:T(8,128)S(1)}, f32[64,4,4,144]{3,1,2,0:T(4,128)S(1)}, f32[64,4,48]{0,2,1:T(8,128)S(1)}, /*index=5*/s32[]{:T(128)}) while((s32[]{:T(128)}, f32[3,8,48,144]{3,2,1,0:T(8,128)S(1)}, f32[3,64,4,8]{1,3,0,2:T(8,128)S(1)}, f32[64,4,4,144]{3,1,2,0:T(4,128)S(1)}, ...), condition=%wide.region_5.6_spmd, body=%wide.region_4.5_spmd.sunk | while | flops 184025088 | bytes 4399181 | solution.py:126
  27.5 2.3 %convolution_bitcast_fusion.4 = f32[64,4,8,144]{3,2,1,0:T(8,128)S(1)} fusion(f32[64,4,4,144]{3,1,2,0:T(4,128)S(1)} %get-tuple-element.224, f32[1,64,4,8]{3,2,1,0:T(4,128)S(1)} %copy.133), kind=kOutput, calls=%fused_computation.4.clone.1 | convolution fusion | flops 14155776 | bytes 1777664 | tf_op jit(solution)/shard_map/while/body/eval_jaxpr/sia,sijc->sjac/dot_general | solution.py:123
  29.8 2.7 %fusion.189 = f32[3,8,48,144]{3,2,1,0:T(8,128)S(1)} fusion(f32[3,8,48,144]{3,2,1,0:T(8,128)S(1)} %get-tuple-element.216, s32[]{:T(128)} %get-tuple-element.215, f32[64,4,8,144]{3,2,1,0:T(8,128)S(1)} %convolution_bitcast_fusion.4, f32[64,4,48]{0,2,1:T(8,128)S(1)} %get-tuple-element.225), kind=kOutput, calls=%fused_computation.6.clone.1 | convolution fusion | flops 169869312 | bytes 2588676 | tf_op jit(solution)/shard_map/while/body/eval_jaxpr/sjb,sjac->abc/dot_general | solution.py:124
  32.6 2.3 %convolution_bitcast_fusion.4 = f32[64,4,8,144]{3,2,1,0:T(8,128)S(1)} fusion(f32[64,4,4,144]{3,1,2,0:T(4,128)S(1)} %get-tuple-element.224, f32[1,64,4,8]{3,2,1,0:T(4,128)S(1)} %copy.133), kind=kOutput, calls=%fused_computation.4.clone.1 | convolution fusion | flops 14155776 | bytes 1777664 | tf_op jit(solution)/shard_map/while/body/eval_jaxpr/sia,sijc->sjac/dot_general | solution.py:123
  34.9 2.7 %fusion.189 = f32[3,8,48,144]{3,2,1,0:T(8,128)S(1)} fusion(f32[3,8,48,144]{3,2,1,0:T(8,128)S(1)} %get-tuple-element.216, s32[]{:T(128)} %get-tuple-element.215, f32[64,4,8,144]{3,2,1,0:T(8,128)S(1)} %convolution_bitcast_fusion.4, f32[64,4,48]{0,2,1:T(8,128)S(1)} %get-tuple-element.225), kind=kOutput, calls=%fused_computation.6.clone.1 | convolution fusion | flops 169869312 | bytes 2588676 | tf_op jit(solution)/shard_map/while/body/eval_jaxpr/sjb,sjac->abc/dot_general | solution.py:124
  37.7 2.3 %convolution_bitcast_fusion.4 = f32[64,4,8,144]{3,2,1,0:T(8,128)S(1)} fusion(f32[64,4,4,144]{3,1,2,0:T(4,128)S(1)} %get-tuple-element.224, f32[1,64,4,8]{3,2,1,0:T(4,128)S(1)} %copy.133), kind=kOutput, calls=%fused_computation.4.clone.1 | convolution fusion | flops 14155776 | bytes 1777664 | tf_op jit(solution)/shard_map/while/body/eval_jaxpr/sia,sijc->sjac/dot_general | solution.py:123
  40.0 2.7 %fusion.189 = f32[3,8,48,144]{3,2,1,0:T(8,128)S(1)} fusion(f32[3,8,48,144]{3,2,1,0:T(8,128)S(1)} %get-tuple-element.216, s32[]{:T(128)} %get-tuple-element.215, f32[64,4,8,144]{3,2,1,0:T(8,128)S(1)} %convolution_bitcast_fusion.4, f32[64,4,48]{0,2,1:T(8,128)S(1)} %get-tuple-element.225), kind=kOutput, calls=%fused_computation.6.clone.1 | convolution fusion | flops 169869312 | bytes 2588676 | tf_op jit(solution)/shard_map/while/body/eval_jaxpr/sjb,sjac->abc/dot_general | solution.py:124
  43.8 1.9 %collective-permute-start.1 = (f32[8,48,144]{2,1,0:T(8,128)S(1)}, f32[8,48,144]{2,1,0:T(8,128)S(1)}, u32[]{:S(2)}, u32[]{:S(2)}) collective-permute-start(f32[8,48,144]{2,1,0:T(8,128)S(1)} %get-tuple-element.163), channel_id=1, source_target_pairs={{8,0},{16,8},{24,16},{0,24},{9,1},{17,9},{25,17},{1,25},{10,2},{18... | collective-permute-start | bytes 663560 | tf_op jit(solution)/shard_map/ppermute | solution.py:27
  45.7 10.0 %collective-permute-done = f32[8,48,144]{2,1,0:T(8,128)S(1)} collective-permute-done((f32[8,48,144]{2,1,0:T(8,128)S(1)}, f32[8,48,144]{2,1,0:T(8,128)S(1)}, u32[]{:S(2)}, u32[]{:S(2)}) %collective-permute-start) | collective-permute-done | bytes 221216 | tf_op jit(solution)/shard_map/ppermute | solution.py:24
  55.7 5.1 %collective-permute-done.1 = f32[8,48,144]{2,1,0:T(8,128)S(1)} collective-permute-done((f32[8,48,144]{2,1,0:T(8,128)S(1)}, f32[8,48,144]{2,1,0:T(8,128)S(1)}, u32[]{:S(2)}, u32[]{:S(2)}) %collective-permute-start.1) | collective-permute-done | bytes 221216 | tf_op jit(solution)/shard_map/ppermute | solution.py:27
  69.6 2.2 %collective-permute-start.5 = (f32[40,64,8]{1,2,0:T(8,128)}, f32[40,64,8]{1,2,0:T(8,128)}, u32[]{:S(2)}, u32[]{:S(2)}) collective-permute-start(f32[40,64,8]{1,2,0:T(8,128)} %copy.85), channel_id=1, source_target_pairs={{1,0},{2,1},{3,2},{0,3},{5,4},{6,5},{7,6},{4,7},{9,8},{10,9},{11,1... | collective-permute-start | bytes 245768 | tf_op jit(solution)/shard_map/ppermute | solution.py:27
  71.9 4.0 %collective-permute-done.4 = f32[40,64,8]{1,2,0:T(8,128)} collective-permute-done((f32[40,64,8]{1,2,0:T(8,128)S(1)}, f32[40,64,8]{1,2,0:T(8,128)}, u32[]{:S(2)}, u32[]{:S(2)}) %collective-permute-start.4) | collective-permute-done | bytes 81952 | tf_op jit(solution)/shard_map/ppermute | solution.py:24
  78.7 2.4 %copy.87 = f32[40,64,8]{2,1,0:T(8,128)} copy(f32[40,64,8]{1,2,0:T(8,128)} %collective-permute-done.5) | data formatting | bytes 163840 | tf_op jit(solution)/shard_map/ppermute | solution.py:27
  81.1 1.9 %fusion.35 = f32[8,64,160]{2,1,0:T(8,128)S(1)} fusion(f32[40,64,8]{2,1,0:T(8,128)} %copy.87, f32[40,64,8]{2,1,0:T(8,128)S(1)} %copy.86, f32[40,8,144]{2,1,0:T(8,128)} %copy-done.2, f32[40,8,144]{2,1,0:T(8,128)} %copy-done.1, f32[8,48,144]{2,1,0:T(8,128)S(1)} %collective-permute-done.1, f32[24,48,144]{2,1,0:T(8,128)S(1)} %bitcast.191, ...), kind=kLoop, calls=%fused_computation.48 | loop fusion | flops 1638400 | bytes 1966080 | tf_op jit(solution)/shard_map/add | solution.py:50
  86.0 4.4 %all-to-all-start.2 = ((f32[8,32,128]{2,0,1:T(8,128)}), f32[8,32,128]{2,0,1:T(8,128)S(1)}, u32[]{:S(2)}, u32[]{:S(2)}) async-start(f32[8,32,128]{2,0,1:T(8,128)} %copy.88), calls=%async_computation.2 | async-start | bytes 262144 | tf_op jit(solution)/shard_map/all_to_all | solution.py:129
  90.3 3.9 %fusion.20 = f32[512,512]{1,0:T(8,128)S(1)} fusion(s32[512]{0:T(512)S(1)} %mul.505), kind=kLoop, calls=%fused_computation.34 | loop fusion | flops 3932160 | bytes 1050624 | tf_op jit(solution)/shard_map/mul | solution.py:66
  94.2 2.0 %all-to-all-done.2 = f32[8,32,128]{2,0,1:T(8,128)S(1)} async-done(((f32[8,32,128]{2,0,1:T(8,128)}), f32[8,32,128]{2,0,1:T(8,128)S(1)}, u32[]{:S(2)}, u32[]{:S(2)}) %all-to-all-start.2) | async-done | bytes 131104 | tf_op jit(solution)/shard_map/all_to_all | solution.py:129
  96.2 4.8 %convolution_negate_fusion = f32[8,8,512]{2,1,0:T(8,128)S(1)} fusion(f32[8,4,8,128]{3,0,2,1:T(8,128)S(1)} %bitcast.204), kind=kOutput, calls=%fused_computation.26 | convolution fusion | flops 205291520 | bytes 262144 | tf_op jit(solution)/shard_map/xyz,zk->xyk/dot_general | solution.py:133
  103.3 3.9 %all_to_all.73 = f32[2,1,32768]{2,1,0:T(1,128)S(1)} all-to-all(f32[2,1,32768]{2,1,0:T(1,128)S(1)} %reshape.1719), channel_id=1, replica_groups=mesh['gx'=4,'gy'=2,'gz'=4] {'gy'}, dimensions={0} | all-to-all | bytes 524288 | tf_op jit(solution)/shard_map/all_to_all | solution.py:142
  109.9 12.2 %all_to_all.74 = f32[4,1,16384]{2,1,0:T(1,128)S(1)} all-to-all(f32[4,1,16384]{2,1,0:T(1,128)S(1)} %reshape.1721), channel_id=1, replica_groups=mesh['gx'=4,'gy'=2,'gz'=4] {'gz'}, dimensions={0} | all-to-all | bytes 524288 | tf_op jit(solution)/shard_map/all_to_all | solution.py:141
  126.7 8.1 %all_to_all.75 = f32[4,1,16384]{2,1,0:T(1,128)S(1)} all-to-all(f32[4,1,16384]{2,1,0:T(1,128)S(1)} %reshape.1723), channel_id=1, replica_groups=mesh['gx'=4,'gy'=2,'gz'=4] {'gx'}, dimensions={0} | all-to-all | bytes 524288 | tf_op jit(solution)/shard_map/all_to_all | solution.py:159
  (109 shorter events, 42.5 us)
Async XLA Ops:
  0.6 9.8 %copy-start = (f32[16]{0:T(128)S(1)}, f32[16]{0:T(128)}, u32[]{:S(2)}) copy-start(f32[16]{0:T(128)} %param.31) | copy-start | bytes 196
  5.2 9.9 %all-to-all-start = ((s32[4,4,16]{2,0,1:T(4,128)}), s32[4,4,16]{2,0,1:T(4,128)S(1)}, u32[]{:S(2)}, u32[]{:S(2)}) async-start(s32[4,4,16]{2,0,1:T(4,128)} %copy.77), calls=%async_computation | async-start | bytes 16384 | tf_op jit(solution)/shard_map/all_to_all | solution.py:96
  15.1 9.0 %all-to-all-start.1 = ((f32[533,4,16]{0,2,1:T(8,128)}), f32[533,4,16]{0,2,1:T(8,128)S(1)}, u32[]{:S(2)}, u32[]{:S(2)}) async-start(f32[533,4,16]{0,2,1:T(8,128)} %bitcast.20), calls=%async_computation.1 | async-start | bytes 327680 | tf_op jit(solution)/shard_map/all_to_all | solution.py:93
  42.7 12.9 %collective-permute-start = (f32[8,48,144]{2,1,0:T(8,128)S(1)}, f32[8,48,144]{2,1,0:T(8,128)S(1)}, u32[]{:S(2)}, u32[]{:S(2)}) collective-permute-start(f32[8,48,144]{2,1,0:T(8,128)S(1)} %get-tuple-element.162), channel_id=1, source_target_pairs={{0,8},{8,16},{16,24},{24,0},{1,9},{9,17},{17,25},{25,1},{2,10},{10... | collective-permute-start | bytes 663560 | tf_op jit(solution)/shard_map/ppermute | solution.py:24
  43.8 17.0 %collective-permute-start.1 = (f32[8,48,144]{2,1,0:T(8,128)S(1)}, f32[8,48,144]{2,1,0:T(8,128)S(1)}, u32[]{:S(2)}, u32[]{:S(2)}) collective-permute-start(f32[8,48,144]{2,1,0:T(8,128)S(1)} %get-tuple-element.163), channel_id=1, source_target_pairs={{8,0},{16,8},{24,16},{0,24},{9,1},{17,9},{25,17},{1,25},{10,2},{18... | collective-permute-start | bytes 663560 | tf_op jit(solution)/shard_map/ppermute | solution.py:27
  60.8 1.7 %collective-permute-start.2 = (f32[40,8,144]{2,1,0:T(8,128)S(1)}, f32[40,8,144]{2,1,0:T(8,128)S(1)}, u32[]{:S(2)}, u32[]{:S(2)}) collective-permute-start(f32[40,8,144]{2,1,0:T(8,128)S(1)} %get-tuple-element.160), channel_id=1, source_target_pairs={{0,4},{4,0},{1,5},{5,1},{2,6},{6,2},{3,7},{7,3},{8,12},{12,8},{9,1... | collective-permute-start | bytes 552968 | tf_op jit(solution)/shard_map/ppermute | solution.py:24
  60.9 2.1 %collective-permute-start.3 = (f32[40,8,144]{2,1,0:T(8,128)S(1)}, f32[40,8,144]{2,1,0:T(8,128)S(1)}, u32[]{:S(2)}, u32[]{:S(2)}) collective-permute-start(f32[40,8,144]{2,1,0:T(8,128)S(1)} %get-tuple-element.161), channel_id=1, source_target_pairs={{4,0},{0,4},{5,1},{1,5},{6,2},{2,6},{7,3},{3,7},{12,8},{8,12},{13,... | collective-permute-start | bytes 552968 | tf_op jit(solution)/shard_map/ppermute | solution.py:27
  62.5 2.7 %copy-start.1 = (f32[40,8,144]{2,1,0:T(8,128)}, f32[40,8,144]{2,1,0:T(8,128)S(1)}, u32[]{:S(2)}) copy-start(f32[40,8,144]{2,1,0:T(8,128)S(1)} %collective-permute-done.2) | copy-start | bytes 552964
  63.0 0.7 copy-start.2
  67.0 9.0 %collective-permute-start.4 = (f32[40,64,8]{1,2,0:T(8,128)S(1)}, f32[40,64,8]{1,2,0:T(8,128)}, u32[]{:S(2)}, u32[]{:S(2)}) collective-permute-start(f32[40,64,8]{1,2,0:T(8,128)S(1)} %copy.84), channel_id=1, source_target_pairs={{0,1},{1,2},{2,3},{3,0},{4,5},{5,6},{6,7},{7,4},{8,9},{9,10},{10,1... | collective-permute-start | bytes 245768 | tf_op jit(solution)/shard_map/ppermute | solution.py:24
  69.6 9.1 %collective-permute-start.5 = (f32[40,64,8]{1,2,0:T(8,128)}, f32[40,64,8]{1,2,0:T(8,128)}, u32[]{:S(2)}, u32[]{:S(2)}) collective-permute-start(f32[40,64,8]{1,2,0:T(8,128)} %copy.85), channel_id=1, source_target_pairs={{1,0},{2,1},{3,2},{0,3},{5,4},{6,5},{7,6},{4,7},{9,8},{10,9},{11,1... | collective-permute-start | bytes 245768 | tf_op jit(solution)/shard_map/ppermute | solution.py:27
  85.2 15.8 %copy-start.3 = (f32[8,32,128]{2,1,0:T(8,128)}, f32[8,32,128]{2,1,0:T(8,128)S(1)}, u32[]{:S(2)}) copy-start(f32[8,32,128]{2,1,0:T(8,128)S(1)} %scatter-add.19) | copy-start | bytes 393220
  86.0 10.3 %all-to-all-start.2 = ((f32[8,32,128]{2,0,1:T(8,128)}), f32[8,32,128]{2,0,1:T(8,128)S(1)}, u32[]{:S(2)}, u32[]{:S(2)}) async-start(f32[8,32,128]{2,0,1:T(8,128)} %copy.88), calls=%async_computation.2 | async-start | bytes 262144 | tf_op jit(solution)/shard_map/all_to_all | solution.py:129
where the time goes:
time: 140 us; the launch traced here: 139 us
  waiting for transfers between devices  29.1 us (21%)
  matrix products  27.9 us (20%)
  blocking collectives  24.2 us (17%)
  starting transfers between devices  20.9 us (15%)
  local copies, waits for them, and re-layouts  19.1 us (14%)
  other arithmetic  16.8 us (12%)
    ppermute x3, waiting for transfers between devices, padded_2(): lax.ppermute(lax.slice_in_dim(block, block.shape[dim] - width, None, axis...  15.1 us
    all_to_all x1, blocking collectives, shards(): lax.all_to_all(lax.all_to_all(split_view, 'gy', split_axis=5, concat_axis...  12.2 us
    all_to_all x1, blocking collectives, shards(): lax.all_to_all(section_y, 'gx', split_axis=2, concat_axis=3, tiled=True)  8.11 us
    dot_general x3, matrix products, planes(): return jnp.einsum('sjb,sjac->abc', along_y, mixed_planes, precision=highest)  7.98 us
    ppermute x3, waiting for transfers between devices, padded_2(): lax.ppermute(lax.slice_in_dim(block, 0, width, axis=dim), axis, backward)  7.02 us
    dot_general x3, matrix products, planes(): jnp.einsum('sia,sijc->sjac', group_x, partial_z, precision=highest)  6.84 us
    all_to_all x1, starting transfers between devices, shards(): lax.all_to_all(routed_labels, 'gx', split_axis=1, concat_axis=1, tiled=True)  5.19 us
    dot_general x1, matrix products, shards(): imag_z = -jnp.einsum('xyz,zk->xyk', depth_local, sine_z, precision=highest)  4.78 us
  transfers between devices with their start and end apart: 9, of which 9 were waited for; matrix products, arithmetic and copies ran while one was open for 8% of the time, Pallas kernels for 0%

commit v1 on v0

v1 whole, which is shorter than its diff:
```python
import functools
import math

import jax
import jax.numpy as jnp
import numpy as np
from jax import lax
from jax.experimental import pallas as pl
from jax.experimental.pallas import tpu as pltpu
from jax.sharding import PartitionSpec as P

DEG = 3
HALO = 8
CX = 8
CY = 32
CZ = 128
SIDE = DEG + 1
LANES = 128
SPAN = 24

highest = lax.Precision.HIGHEST
f32 = jnp.float32
bf16 = jnp.bfloat16


def iota_f(shape, dim):
    return lax.broadcasted_iota(jnp.int32, shape, dim).astype(f32)


def cos_sin(turns):
    r = turns - jnp.floor(turns + 0.5)
    t = r * math.pi
    t2 = t * t
    s = t * _poly(t2, [(-1) ** n / math.factorial(2 * n + 1) for n in range(7)])
    c = _poly(t2, [(-1) ** n / math.factorial(2 * n) for n in range(8)])
    return 1.0 - 2.0 * s * s, 2.0 * s * c


def _poly(x, coefs):
    out = jnp.full_like(x, coefs[-1])
    for a in reversed(coefs[:-1]):
        out = out * x + a
    return out


def wrapped(cells, centre, total):
    d = cells - centre
    d = jnp.where(d < -HALO, d + total, d)
    return jnp.where(d > total - 1 - HALO, d - total, d)


def factors(offset, within, rate, radius):
    u = offset - within
    env = jnp.exp(-rate * u * u) * (jnp.abs(offset) <= radius).astype(f32)
    s = u * (1.0 / HALO)
    out = [env]
    for _ in range(DEG):
        out.append(out[-1] * s)
    return out


def split(v):
    hi = v.astype(bf16)
    return hi, (v - hi.astype(f32)).astype(bf16)


def nt(a, b):
    return lax.dot_general(a, b, (((1,), (1,)), ((), ())), preferred_element_type=f32)


def spectral(frequency, length, centre, within, rate, radius, table):
    n = frequency.shape[0]
    offs = iota_f((SPAN, LANES), 0) - HALO
    four = jnp.concatenate(factors(offs, within, rate, radius), axis=1)
    part = jnp.dot(table, four, precision=highest, preferred_element_type=f32)
    pc, ps = cos_sin(frequency * centre * (1.0 / length))
    out = []
    for d in range(SIDE):
        a = part[:n, d * LANES : (d + 1) * LANES]
        b = part[n:, d * LANES : (d + 1) * LANES]
        out.append((a * pc + b * ps, b * pc - a * ps))
    return out


def span_table(frequency, length):
    offs = iota_f((1, SPAN), 1) - HALO
    c, s = cos_sin(frequency * offs * (1.0 / length))
    return jnp.concatenate([c, -s], axis=0)


def chunk_work(prm, sizes, place, refs, first):
    nx, ny, nz, nky, nkz = sizes
    gx, gy, gz, kz0 = place
    (h_s, hd_s, fxl_s, t_hi, t_lo, d_hi, d_lo, z_s, zd_s, ytab, ztab, acc, acc_lo, dacc, dacc_lo) = refs
    rows = lambda a: prm[a : a + 1, :]
    base = SIDE**3
    cx, cy, cz, ox, oy, oz, rate, radius = [rows(base + n) for n in range(8)]
    kyc = iota_f((nky, 1), 0) + (gx * nky).astype(f32)
    kzc = iota_f((nkz, 1), 0) + (kz0 * nkz).astype(f32)
    fy = spectral(kyc, ny, cy, oy, rate, radius, ytab[...])
    fz = spectral(kzc, nz, cz, oz, rate, radius, ztab[...])
    fx = factors(wrapped(iota_f((nx, LANES), 0), cx, float(nx)), ox, rate, radius)
    fyl = factors(
        wrapped(iota_f((CY, LANES), 0) + (gy * CY).astype(f32), cy, float(ny)), oy, rate, radius
    )
    fzl = factors(
        wrapped(iota_f((CZ, LANES), 0) + (gz * CZ).astype(f32), cz, float(nz)), oz, rate, radius
    )
    fxl = factors(
        wrapped(iota_f((CX, LANES), 0) + (gx * CX).astype(f32), cx, float(nx)), ox, rate, radius
    )
    for i in range(SIDE):
        fxl_s[i] = fxl[i]
    for k in range(SIDE):
        lanes = slice(k * LANES, (k + 1) * LANES)
        zhi, zlo = split(jnp.concatenate(fz[k], axis=0))
        z_s[: 2 * nkz, lanes] = zhi
        z_s[2 * nkz :, lanes] = zlo
        zhi, zlo = split(fzl[k])
        zd_s[:CZ, lanes] = zhi
        zd_s[CZ:, lanes] = zlo
        for i in range(SIDE):
            re = im = de = None
            for j in range(SIDE):
                c = rows((i * SIDE + j) * SIDE + k)
                re = c * fy[j][0] if re is None else re + c * fy[j][0]
                im = c * fy[j][1] if im is None else im + c * fy[j][1]
                de = c * fyl[j] if de is None else de + c * fyl[j]
            h_s[k * SIDE + i, :nky] = re
            h_s[k * SIDE + i, nky:] = im
            hd_s[k * SIDE + i] = de
    group = 4

    def mix(g, carry):
        for rr in range(group):
            r = g * group + rr
            for k in range(SIDE):
                v = None
                for i in range(SIDE):
                    w = h_s[k * SIDE + i, pl.ds(r, 1), :] * fx[i]
                    v = w if v is None else v + w
                hi, lo = split(v)
                t_hi[pl.ds(pl.multiple_of(r * nx, nx), nx), k * LANES : (k + 1) * LANES] = hi
                t_lo[pl.ds(pl.multiple_of(r * nx, nx), nx), k * LANES : (k + 1) * LANES] = lo
        return carry

    lax.fori_loop(0, 2 * nky // group, mix, 0)
    for k in range(SIDE):
        for x in range(CX):
            v = None
            for i in range(SIDE):
                w = hd_s[k * SIDE + i] * fxl_s[i, x : x + 1, :]
                v = w if v is None else v + w
            hi, lo = split(v)
            d_hi[x * CY : (x + 1) * CY, k * LANES : (k + 1) * LANES] = hi
            d_lo[x * CY : (x + 1) * CY, k * LANES : (k + 1) * LANES] = lo
    block = 256
    for b in range(2 * nky * nx // block):
        s = slice(b * block, (b + 1) * block)
        acc[s] = acc[s] + nt(t_hi[s], z_s[...])
        acc_lo[s] = acc_lo[s] + nt(t_lo[s], z_s[: 2 * nkz])
    dacc[...] = dacc[...] + nt(d_hi[...], zd_s[...])
    dacc_lo[...] = dacc_lo[...] + nt(d_lo[...], zd_s[:CZ])


def finish(sizes, acc, acc_lo, dacc, dacc_lo, xtab, dens_ref, spec_ref):
    nx, ny, nz, nky, nkz = sizes
    dens_ref[...] = dacc[:, :CZ] + dacc[:, CZ:] + dacc_lo[...]
    wide = max(nx, LANES)
    per = wide // nx
    for g in range(nky // per):

        def take(r0):
            s = slice(r0, r0 + wide)
            v = acc[s, : 2 * nkz] + acc[s, 2 * nkz :] + acc_lo[s]
            return v.T

        re = take(g * wide)
        im = take(nky * nx + g * wide)
        c_re = re[:nkz] - im[nkz:]
        c_im = re[nkz:] + im[:nkz]
        both = jnp.concatenate([c_re, c_im], axis=0)
        q = jnp.dot(both, xtab[...], precision=highest, preferred_element_type=f32)
        spec_ref[0, :, g * wide : (g + 1) * wide] = q[:nkz, :wide] + q[nkz:, wide:]
        spec_ref[1, :, g * wide : (g + 1) * wide] = q[nkz:, :wide] - q[:nkz, wide:]


def scratches(sizes):
    nx, ny, nz, nky, nkz = sizes
    m = 2 * nky * nx
    k = SIDE * LANES
    return [
        pltpu.VMEM((SIDE * SIDE, 2 * nky, LANES), f32),
        pltpu.VMEM((SIDE * SIDE, CY, LANES), f32),
        pltpu.VMEM((SIDE, CX, LANES), f32),
        pltpu.VMEM((m, k), bf16),
        pltpu.VMEM((m, k), bf16),
        pltpu.VMEM((CX * CY, k), bf16),
        pltpu.VMEM((CX * CY, k), bf16),
        pltpu.VMEM((4 * nkz, k), bf16),
        pltpu.VMEM((2 * CZ, k), bf16),
        pltpu.VMEM((2 * nky, SPAN), f32),
        pltpu.VMEM((2 * nkz, SPAN), f32),
        pltpu.VMEM((m, 4 * nkz), f32),
        pltpu.VMEM((m, 2 * nkz), f32),
        pltpu.VMEM((CX * CY, 2 * CZ), f32),
        pltpu.VMEM((CX * CY, CZ), f32),
    ]


def start_work(sizes, place, refs):
    nx, ny, nz, nky, nkz = sizes
    gx, gy, gz, kz0 = place
    ytab, ztab, acc, acc_lo, dacc, dacc_lo = refs[-6:]
    kyc = iota_f((nky, 1), 0) + (gx * nky).astype(f32)
    kzc = iota_f((nkz, 1), 0) + (kz0 * nkz).astype(f32)
    ytab[...] = span_table(kyc, ny)
    ztab[...] = span_table(kzc, nz)
    for r in (acc, acc_lo, dacc, dacc_lo):
        r[...] = jnp.zeros_like(r)


def where_am_i():
    gx, gy, gz = (lax.axis_index(a) for a in ("gx", "gy", "gz"))
    return gx, gy, gz, gy * lax.axis_size("gz") + gz


def kernel(sizes, prm_ref, xtab, dens_ref, spec_ref, *refs):
    place = where_am_i()
    start_work(sizes, place, refs)

    def step(c, carry):
        prm = prm_ref[:, pl.ds(pl.multiple_of(c * LANES, LANES), LANES)]
        chunk_work(prm, sizes, place, refs, None)
        return carry

    lax.fori_loop(0, prm_ref.shape[1] // LANES, step, 0)
    finish(sizes, *refs[-4:], xtab, dens_ref, spec_ref)


def x_table(nx, total):
    wide = max(nx, LANES)
    idx = np.arange(nx)
    angle = (idx[:, None] * idx[None, :] % nx) * (2.0 * math.pi / nx)
    eye = np.eye(wide // nx)
    scale = 1.0 / math.sqrt(total)
    return np.concatenate(
        [np.kron(eye, np.cos(angle)), np.kron(eye, np.sin(angle))], axis=1
    ).astype(np.float32) * np.float32(scale)


def shards(
    pair_blocks, basis_map, pair_cells, pair_offsets, exponent_index, radius_index, exponents
):
    n_gx, n_gy, n_gz = (lax.axis_size(a) for a in ("gx", "gy", "gz"))
    nx, ny, nz = CX * n_gx, CY * n_gy, CZ * n_gz
    sizes = (nx, ny, nz, ny // n_gx, nz // (n_gy * n_gz))
    nky, nkz = sizes[3:]
    selector = (
        exponent_index[None, :] == jnp.arange(exponents.shape[0], dtype=jnp.int32)[:, None]
    ).astype(f32)
    radius = (HALO - radius_index).astype(f32)
    rate = jnp.sum(exponents[:, None] * selector, axis=0) / (radius * radius)
    coefs = jnp.dot(basis_map.T, pair_blocks, precision=highest)
    prm = jnp.concatenate(
        [coefs, pair_cells.astype(f32), pair_offsets, rate[None], radius[None]], axis=0
    )
    prm = lax.all_gather(prm, ("gx", "gy", "gz"), axis=1, tiled=True)
    dens, spec = pl.pallas_call(
        functools.partial(kernel, sizes),
        out_shape=[
            jax.ShapeDtypeStruct((CX * CY, CZ), f32),
            jax.ShapeDtypeStruct((2, nkz, nky * nx), f32),
        ],
        in_specs=[pl.BlockSpec(memory_space=pltpu.VMEM)] * 2,
        out_specs=[pl.BlockSpec(memory_space=pltpu.VMEM)] * 2,
        scratch_shapes=scratches(sizes),
    )(prm, jnp.asarray(x_table(nx, nx * ny * nz)))
    return dens.reshape(CX, CY, CZ), spec.reshape(2, nkz, nky, nx)


def solution(mesh):
    placed = (
        P(None, ("gx", "gy", "gz")),
        P(),
        P(None, ("gx", "gy", "gz")),
        P(None, ("gx", "gy", "gz")),
        P(("gx", "gy", "gz")),
        P(("gx", "gy", "gz")),
        P(),
    )
    return jax.shard_map(
        shards,
        mesh=mesh,
        in_specs=placed,
        out_specs=(P("gx", "gy", "gz"), P(None, ("gy", "gz"), "gx", None)),
        check_vma=False,
    )
```

time: 140 us -> 103 us (0.74)
  blocking collectives: 24.2 us -> 73.9 us
  waiting for transfers between devices: 29.1 us -> 0 us
  matrix products: 27.9 us -> 1.17 us
  Pallas kernels: 0 us -> 22.2 us
  starting transfers between devices: 20.9 us -> 0 us
  other arithmetic: 16.8 us -> 0.82 us
  local copies, waits for them, and re-layouts: 19.1 us -> 3.95 us
    all_gather x0 -> x1, blocking collectives: none -> 73.9 us  [shards(): prm = lax.all_gather(prm, ('gx', 'gy', 'gz'), axis=1, tiled=True)]
    dot_general x19 -> x1, matrix products: 27.9 us -> 1.17 us  [shards(): coefs = jnp.dot(basis_map.T, pair_blocks, precision=highest)]
    all_to_all x3 -> x0, blocking collectives: 24.2 us -> none  [the longest x1 12.2 us: shards(): lax.all_to_all(lax.all_to_all(split_view, 'gy', split_axis=5, concat_axis...]
    pallas_call x0 -> x1, Pallas kernels: none -> 22.2 us  [shards(): pl.pallas_call(functools.partial(kernel, sizes), out_shape=[jax.ShapeDtyp...]
    ppermute x6 -> x0, waiting for transfers between devices: 22.1 us -> none  [the longest x3 15.1 us: padded_2(): lax.ppermute(lax.slice_in_dim(block, block.shape[dim] - width, None, axis...]
    all_to_all x3 -> x0, starting transfers between devices: 13.5 us -> none  [the longest x1 5.19 us: shards(): lax.all_to_all(routed_labels, 'gx', split_axis=1, concat_axis=1, tiled=True)]
    ppermute x6 -> x0, starting transfers between devices: 7.39 us -> none  [the longest x3 4.67 us: padded_2(): lax.ppermute(lax.slice_in_dim(block, 0, width, axis=dim), axis, backward)]
    all_to_all x3 -> x0, waiting for transfers between devices: 7.02 us -> none  [the longest x1 4.74 us: shards(): lax.all_to_all(outgoing.reshape(-1, x_devices, capacity), 'gx', split_axi...]
  transfers between devices with their start and end apart: 9 -> 0, of which waited for: 9 -> 0; matrix products, arithmetic and copies ran while one was open for 8% -> 0% of each run, Pallas kernels for 0% -> 0%
where the time goes in v1:
time: 103 us
  blocking collectives  73.9 us (72%)
  Pallas kernels  22.2 us (22%)
  local copies, waits for them, and re-layouts  3.95 us (4%)
  matrix products  1.17 us (1%)
    all_gather x1, blocking collectives, shards(): prm = lax.all_gather(prm, ('gx', 'gy', 'gz'), axis=1, tiled=True)  73.9 us
    pallas_call x1, Pallas kernels, shards(): pl.pallas_call(functools.partial(kernel, sizes), out_shape=[jax.ShapeDtyp...  22.2 us

profile of v1, /device:TPU:0, one launch (start us, length us, event | category | flops | bytes accessed | tf_op | source)
XLA Modules:
  0.0 102.8 jit_solution(3134860309294767147)
XLA Ops:
  0.6 0.0 copy-start
  0.6 0.0 copy-start.3
  0.7 0.8 select_reduce_fusion
  1.5 0.0 copy-done.3
  1.5 0.0 copy-start.2
  1.5 0.6 copy-done.2
  2.1 0.1 copy.20
  2.2 0.1 copy.23
  2.3 0.1 copy.22
  2.4 0.0 copy-done
  2.4 0.0 copy-start.1
  2.4 1.2 %fusion.1 = f32[64,32]{0,1:T(8,128)S(1)} fusion(f32[529,64]{0,1:T(8,128)S(1)} %copy-done, f32[529,32]{0,1:T(8,128)} %param.8), kind=kOutput, calls=%fused_computation.5 | convolution fusion | flops 13000704 | bytes 211328 | tf_op jit(solution)/shard_map/dot_general | solution.py:264
  3.6 0.0 copy-done.1
  3.6 0.1 copy.21
  3.7 0.1 concatenate.3
  3.8 73.9 %all_gather.3 = f32[72,1024]{0,1:T(8,128)S(1)} all-gather(f32[72,32]{0,1:T(8,128)S(1)} %concatenate.3), channel_id=1, replica_groups=mesh['gx'=4,'gy'=2,'gz'=4] {'gx','gy','gz'}, dimensions={1}, use_global_device_ids=true | all-gather | bytes 304128 | tf_op jit(solution)/shard_map/all_gather | solution.py:268
  77.7 0.9 copy.24.prm_ref
  78.6 22.2 %shard_map.95 = (f32[256,128]{1,0:T(8,128)}, f32[2,64,512]{2,1,0:T(8,128)}) custom-call(f32[72,1024]{1,0:T(8,128)} %copy.24.prm_ref, f32[128,256]{1,0:T(8,128)} %constant.7.clone.xtab), custom_call_target="tpu_custom_call" | custom-call | tf_op jit(solution)/shard_map/pallas_call | solution.py:269
  100.9 1.9 %copy.25 = f32[2,64,512]{1,2,0:T(8,128)} copy(f32[2,64,512]{2,1,0:T(8,128)} %get-tuple-element.5) | data formatting | bytes 524288 | tf_op jit(solution)/shard_map/pallas_call | solution.py:269
  (3 shorter events, 0.0 us)
Async XLA Ops:
  0.6 1.8 %copy-start = (f32[529,64]{0,1:T(8,128)S(1)}, f32[529,64]{0,1:T(8,128)}, u32[]{:S(2)}) copy-start(f32[529,64]{0,1:T(8,128)} %param.9) | copy-start | bytes 406276
  0.6 0.8 copy-start.3
  1.5 0.7 copy-start.2
  2.4 1.2 %copy-start.1 = (f32[3,32]{1,0:T(4,128)S(1)}, f32[3,32]{1,0:T(4,128)}, u32[]{:S(2)}) copy-start(f32[3,32]{1,0:T(4,128)} %param.11) | copy-start | bytes 1156

commit v2 on v1

--- a/solution.py
+++ b/solution.py
@@ -88,7 +88,7 @@
     return jnp.concatenate([c, -s], axis=0)
 
 
-def chunk_work(prm, sizes, place, refs, first):
+def chunk_work(prm, sizes, place, refs):
     nx, ny, nz, nky, nkz = sizes
     gx, gy, gz, kz0 = place
     (h_s, hd_s, fxl_s, t_hi, t_lo, d_hi, d_lo, z_s, zd_s, ytab, ztab, acc, acc_lo, dacc, dacc_lo) = refs
@@ -225,17 +225,95 @@
     return gx, gy, gz, gy * lax.axis_size("gz") + gz
 
 
-def kernel(sizes, prm_ref, xtab, dens_ref, spec_ref, *refs):
+def unpack(blocks, prm):
+    owner = lax.broadcasted_iota(jnp.int32, (SPAN, LANES), 1) // (LANES // len(blocks))
+    for g in range(prm.shape[0] // SPAN):
+        v = None
+        for d, block in enumerate(blocks):
+            shift = (d - g) % len(blocks) * (LANES // len(blocks))
+            w = pltpu.roll(block, shift, 1) if shift else block
+            v = w if v is None else jnp.where(owner == d, w, v)
+        prm[g * SPAN : (g + 1) * SPAN] = v
+
+
+def kernel(sizes, counts, own_ref, xtab, dens_ref, spec_ref, prm, cols, *refs):
+    refs, (send_z, recv_z, send_c, recv_c) = refs[:-4], refs[-4:]
+    n_gx, n_gy, n_gz = counts
     place = where_am_i()
+    gx, gy, gz = place[:3]
+    n_col = n_gx * n_gy
+
+    def along_z(r):
+        return gx, gy, lax.rem(gz + n_gz - r, n_gz)
+
+    def column(c):
+        dx, dy = c // n_gy, c % n_gy
+        return lax.rem(gx + n_gx - dx, n_gx), lax.rem(gy + n_gy - dy, n_gy), gz
+
+    mesh_type = pl.DeviceIdType.MESH
+    barrier = pltpu.get_barrier_semaphore()
+    for r in range(1, n_gz):
+        pl.semaphore_signal(barrier, inc=1, device_id=along_z(r), device_id_type=mesh_type)
+
+    def greet(c, carry):
+        pl.semaphore_signal(barrier, inc=1, device_id=column(c), device_id_type=mesh_type)
+        return carry
+
+    lax.fori_loop(1, n_col, greet, 0)
+    cols[0, 0] = own_ref[...]
     start_work(sizes, place, refs)
+    pl.semaphore_wait(barrier, n_gz + n_col - 2)
+
+    def copy_z(r):
+        return pltpu.make_async_remote_copy(
+            src_ref=own_ref,
+            dst_ref=cols.at[0, r],
+            send_sem=send_z.at[r],
+            recv_sem=recv_z.at[r],
+            device_id=along_z(r),
+            device_id_type=mesh_type,
+        )
+
+    def copy_c(c):
+        return pltpu.make_async_remote_copy(
+            src_ref=cols.at[0],
+            dst_ref=cols.at[c],
+            send_sem=send_c.at[c],
+            recv_sem=recv_c.at[c],
+            device_id=column(c),
+            device_id_type=mesh_type,
+        )
+
+    for r in range(1, n_gz):
+        copy_z(r).start()
+    for r in range(1, n_gz):
+        copy_z(r).wait_recv()
+
+    def send(c, carry):
+        copy_c(c).start()
+        return carry
+
+    lax.fori_loop(1, n_col, send, 0)
 
     def step(c, carry):
-        prm = prm_ref[:, pl.ds(pl.multiple_of(c * LANES, LANES), LANES)]
-        chunk_work(prm, sizes, place, refs, None)
-        return carry
-
-    lax.fori_loop(0, prm_ref.shape[1] // LANES, step, 0)
+        @pl.when(c > 0)
+        def _():
+            copy_c(c).wait_recv()
+
+        unpack([cols[c, r] for r in range(n_gz)], prm)
+        chunk_work(prm, sizes, place, refs)
+        return carry
+
+    lax.fori_loop(0, n_col, step, 0)
     finish(sizes, *refs[-4:], xtab, dens_ref, spec_ref)
+    for r in range(1, n_gz):
+        copy_z(r).wait_send()
+
+    def drain(c, carry):
+        copy_c(c).wait_send()
+        return carry
+
+    lax.fori_loop(1, n_col, drain, 0)
 
 
 def x_table(nx, total):
@@ -265,17 +343,31 @@
     prm = jnp.concatenate(
         [coefs, pair_cells.astype(f32), pair_offsets, rate[None], radius[None]], axis=0
     )
-    prm = lax.all_gather(prm, ("gx", "gy", "gz"), axis=1, tiled=True)
+    pair_dev = prm.shape[1]
+    assert prm.shape[0] == 3 * SPAN and n_gz * pair_dev == LANES and n_gz >= 3
+    groups = [prm[g * SPAN : (g + 1) * SPAN] for g in range(3)]
+    groups.append(jnp.zeros((SPAN, LANES - 3 * pair_dev), f32))
+    own = jnp.concatenate(groups, axis=1)
+    n_col = n_gx * n_gy
     dens, spec = pl.pallas_call(
-        functools.partial(kernel, sizes),
+        functools.partial(kernel, sizes, (n_gx, n_gy, n_gz)),
         out_shape=[
             jax.ShapeDtypeStruct((CX * CY, CZ), f32),
             jax.ShapeDtypeStruct((2, nkz, nky * nx), f32),
         ],
         in_specs=[pl.BlockSpec(memory_space=pltpu.VMEM)] * 2,
         out_specs=[pl.BlockSpec(memory_space=pltpu.VMEM)] * 2,
-        scratch_shapes=scratches(sizes),
-    )(prm, jnp.asarray(x_table(nx, nx * ny * nz)))
+        scratch_shapes=[
+            pltpu.VMEM((3 * SPAN, LANES), f32),
+            pltpu.VMEM((n_col, n_gz, SPAN, LANES), f32),
+            *scratches(sizes),
+            pltpu.SemaphoreType.DMA((n_gz,)),
+            pltpu.SemaphoreType.DMA((n_gz,)),
+            pltpu.SemaphoreType.DMA((n_col,)),
+            pltpu.SemaphoreType.DMA((n_col,)),
+        ],
+        compiler_params=pltpu.CompilerParams(collective_id=0, has_side_effects=True),
+    )(own, jnp.asarray(x_table(nx, nx * ny * nz)))
     return dens.reshape(CX, CY, CZ), spec.reshape(2, nkz, nky, nx)
 
 

time: 103 us -> 40.1 us (0.39)
  blocking collectives: 73.9 us -> 0 us
  Pallas kernels: 22.2 us -> 32.4 us
    all_gather x1 -> x0, blocking collectives: 73.9 us -> none  [shards(): prm = lax.all_gather(prm, ('gx', 'gy', 'gz'), axis=1, tiled=True)]
    pallas_call x1, Pallas kernels: 22.2 us -> 32.4 us  [shards(): pl.pallas_call(functools.partial(kernel, sizes, (n_gx, n_gy, n_gz)), out_...]
    unnamed x9 -> x11, local copies, waits for them, and re-layouts: 0.76 us -> 1.94 us
where the time goes in v2:
time: 40.1 us; the launch traced here: 39.8 us
  Pallas kernels  32.4 us (81%)
  local copies, waits for them, and re-layouts  4.04 us (10%)
  other arithmetic  1.49 us (4%)
  matrix products  1.15 us (3%)
  between operations  0.72 us (2%)
    pallas_call x1, Pallas kernels, shards(): pl.pallas_call(functools.partial(kernel, sizes, (n_gx, n_gy, n_gz)), out_...  32.4 us
    pallas_call x1, local copies, waits for them, and re-layouts, shards(): pl.pallas_call(functools.partial(kernel, sizes, (n_gx, n_gy, n_gz)), out_...  1.98 us
    unnamed x11, local copies, waits for them, and re-layouts  1.94 us
    dot_general x1, matrix products, shards(): coefs = jnp.dot(basis_map.T, pair_blocks, precision=highest)  1.15 us

profile of v2, /device:TPU:0, one launch (start us, length us, event | category | flops | bytes accessed | tf_op | source)
XLA Modules:
  0.0 39.8 jit_solution(18341922639369982836)
XLA Ops:
  0.6 0.0 copy-start
  0.6 0.0 copy-start.4
  0.7 0.8 %select_reduce_fusion = f32[32]{0:T(128)S(1)} fusion(f32[16]{0:T(128)} %param.14, s32[32]{0:T(128)} %param.12), kind=kLoop, calls=%fused_computation.1 | loop fusion | flops 1504 | bytes 320 | tf_op jit(solution)/shard_map/reduce_sum | solution.py:341
  1.5 0.0 copy-done.4
  1.5 0.0 copy-start.3
  1.5 0.1 pad.3.clone
  1.6 0.6 %copy-done.3 = s32[3,32]{1,0:T(4,128)S(1)} copy-done((s32[3,32]{1,0:T(4,128)S(1)}, s32[3,32]{1,0:T(4,128)}, u32[]{:S(2)}) %copy-start.3) | copy-done | bytes 408
  2.2 0.0 copy-done
  2.2 1.2 %fusion.2 = f32[64,32]{1,0:T(8,128)S(1)} fusion(f32[529,64]{0,1:T(8,128)S(1)} %copy-done, f32[529,32]{0,1:T(8,128)} %param.8), kind=kOutput, calls=%fused_computation.7 | convolution fusion | flops 13000704 | bytes 211328 | tf_op jit(solution)/shard_map/dot_general | solution.py:342
  3.4 0.0 copy-start.2
  3.4 0.7 %copy-done.2 = f32[3,32]{1,0:T(4,128)S(1)} copy-done((f32[3,32]{1,0:T(4,128)S(1)}, f32[3,32]{1,0:T(4,128)}, u32[]{:S(2)}) %copy-start.2) | copy-done | bytes 408
  4.1 0.7 %maximum_maximum_fusion.own_ref = f32[24,128]{1,0:T(8,128)} fusion(f32[24,32]{1,0:T(8,128)S(1)} %slice.14, f32[24,32]{1,0:T(8,128)S(1)} %get-tuple-element.9, f32[24,32]{1,0:T(8,128)S(1)} %get-tuple-element.8, f32[128]{0:T(128)S(1)} %pad.3.clone), kind=kLoop, calls=%fused_computation | loop fusion | flops 9216 | bytes 22016 | tf_op jit(solution)/shard_map/concatenate | solution.py:350
  4.7 32.4 %shard_map.95 = (f32[256,128]{1,0:T(8,128)}, f32[2,64,512]{2,1,0:T(8,128)}) custom-call(f32[24,128]{1,0:T(8,128)} %maximum_maximum_fusion.own_ref, f32[128,256]{1,0:T(8,128)} %constant.8.clone.xtab), custom_call_target="tpu_custom_call" | custom-call | tf_op jit(solution)/shard_map/pallas_call | solution.py:352
  37.1 0.0 copy-start.1
  37.1 2.0 %copy.29 = f32[2,64,512]{1,2,0:T(8,128)} copy(f32[2,64,512]{2,1,0:T(8,128)} %get-tuple-element.5) | data formatting | bytes 524288 | tf_op jit(solution)/shard_map/pallas_call | solution.py:352
  39.1 0.0 copy-done.1
  39.1 0.7 %copy.32 = f32[8,32,128]{2,1,0:T(8,128)} copy(f32[8,32,128]{2,1,0:T(8,128)S(1)} %bitcast.9) | data formatting | bytes 262144
  (7 shorter events, 0.1 us)
Async XLA Ops:
  0.6 1.5 %copy-start = (f32[529,64]{0,1:T(8,128)S(1)}, f32[529,64]{0,1:T(8,128)}, u32[]{:S(2)}) copy-start(f32[529,64]{0,1:T(8,128)} %param.9) | copy-start | bytes 406276
  0.6 0.8 %copy-start.4 = (s32[32]{0:T(128)S(1)}, s32[32]{0:T(128)}, u32[]{:S(2)}) copy-start(s32[32]{0:T(128)} %param.13) | copy-start | bytes 388
  1.5 0.7 %copy-start.3 = (s32[3,32]{1,0:T(4,128)S(1)}, s32[3,32]{1,0:T(4,128)}, u32[]{:S(2)}) copy-start(s32[3,32]{1,0:T(4,128)} %param.10) | copy-start | bytes 1156
  3.4 0.7 %copy-start.2 = (f32[3,32]{1,0:T(4,128)S(1)}, f32[3,32]{1,0:T(4,128)}, u32[]{:S(2)}) copy-start(f32[3,32]{1,0:T(4,128)} %param.11) | copy-start | bytes 1156
  37.1 2.0 %copy-start.1 = (f32[256,128]{1,0:T(8,128)S(1)}, f32[256,128]{1,0:T(8,128)}, u32[]{:S(2)}) copy-start(f32[256,128]{1,0:T(8,128)} %get-tuple-element.4) | copy-start | bytes 393220

commit v3 on v2

--- a/solution.py
+++ b/solution.py
@@ -16,7 +16,8 @@
 CZ = 128
 SIDE = DEG + 1
 LANES = 128
-SPAN = 24
+SPAN = 32
+GROUP = 24
 
 highest = lax.Precision.HIGHEST
 f32 = jnp.float32
@@ -72,7 +73,10 @@
     n = frequency.shape[0]
     offs = iota_f((SPAN, LANES), 0) - HALO
     four = jnp.concatenate(factors(offs, within, rate, radius), axis=1)
-    part = jnp.dot(table, four, precision=highest, preferred_element_type=f32)
+    hi, lo = split(four)
+    part = jnp.dot(
+        table, jnp.concatenate([hi, lo, hi], axis=0), preferred_element_type=f32
+    )
     pc, ps = cos_sin(frequency * centre * (1.0 / length))
     out = []
     for d in range(SIDE):
@@ -85,13 +89,14 @@
 def span_table(frequency, length):
     offs = iota_f((1, SPAN), 1) - HALO
     c, s = cos_sin(frequency * offs * (1.0 / length))
-    return jnp.concatenate([c, -s], axis=0)
+    hi, lo = split(jnp.concatenate([c, -s], axis=0))
+    return jnp.concatenate([hi, hi, lo], axis=1)
 
 
 def chunk_work(prm, sizes, place, refs):
     nx, ny, nz, nky, nkz = sizes
     gx, gy, gz, kz0 = place
-    (h_s, hd_s, fxl_s, t_hi, t_lo, d_hi, d_lo, z_s, zd_s, ytab, ztab, acc, acc_lo, dacc, dacc_lo) = refs
+    (h_s, hd_s, fxl_s, t_hi, t_lo, d_hi, d_lo, z_s, zd_s, ytab, ztab, acc, dacc) = refs
     rows = lambda a: prm[a : a + 1, :]
     base = SIDE**3
     cx, cy, cz, ox, oy, oz, rate, radius = [rows(base + n) for n in range(8)]
@@ -129,24 +134,18 @@
             h_s[k * SIDE + i, :nky] = re
             h_s[k * SIDE + i, nky:] = im
             hd_s[k * SIDE + i] = de
-    group = 4
-
-    def mix(g, carry):
-        for rr in range(group):
-            r = g * group + rr
-            for k in range(SIDE):
-                v = None
-                for i in range(SIDE):
-                    w = h_s[k * SIDE + i, pl.ds(r, 1), :] * fx[i]
-                    v = w if v is None else v + w
-                hi, lo = split(v)
-                t_hi[pl.ds(pl.multiple_of(r * nx, nx), nx), k * LANES : (k + 1) * LANES] = hi
-                t_lo[pl.ds(pl.multiple_of(r * nx, nx), nx), k * LANES : (k + 1) * LANES] = lo
-        return carry
-
-    lax.fori_loop(0, 2 * nky // group, mix, 0)
-    for k in range(SIDE):
-        for x in range(CX):
+    def build(r):
+        for k in range(SIDE):
+            v = None
+            for i in range(SIDE):
+                w = h_s[k * SIDE + i, r : r + 1, :] * fx[i]
+                v = w if v is None else v + w
+            hi, lo = split(v)
+            t_hi[r * nx : (r + 1) * nx, k * LANES : (k + 1) * LANES] = hi
+            t_lo[r * nx : (r + 1) * nx, k * LANES : (k + 1) * LANES] = lo
+
+    def build_cell(x):
+        for k in range(SIDE):
             v = None
             for i in range(SIDE):
                 w = hd_s[k * SIDE + i] * fxl_s[i, x : x + 1, :]
@@ -154,35 +153,44 @@
             hi, lo = split(v)
             d_hi[x * CY : (x + 1) * CY, k * LANES : (k + 1) * LANES] = hi
             d_lo[x * CY : (x + 1) * CY, k * LANES : (k + 1) * LANES] = lo
+
+    def add(target, hi, lo, z, s, n):
+        if n % LANES == 0:
+            both = nt(hi[s], z[...])
+            more = both[:, :n] + both[:, n:]
+        else:
+            more = nt(hi[s], z[:n]) + nt(hi[s], z[n:])
+        target[s] = target[s] + (more + nt(lo[s], z[:n]))
+
     block = 256
-    for b in range(2 * nky * nx // block):
-        s = slice(b * block, (b + 1) * block)
-        acc[s] = acc[s] + nt(t_hi[s], z_s[...])
-        acc_lo[s] = acc_lo[s] + nt(t_lo[s], z_s[: 2 * nkz])
-    dacc[...] = dacc[...] + nt(d_hi[...], zd_s[...])
-    dacc_lo[...] = dacc_lo[...] + nt(d_lo[...], zd_s[:CZ])
-
-
-def finish(sizes, acc, acc_lo, dacc, dacc_lo, xtab, dens_ref, spec_ref):
+    per = max(block // nx, 1)
+    block = per * nx
+    for x in range(CX):
+        build_cell(x)
+    late = [lambda: add(dacc, d_hi, d_lo, zd_s, slice(0, CX * CY), CZ)]
+    for b in range(2 * nky // per):
+        for r in range(b * per, (b + 1) * per):
+            build(r)
+        late.pop()()
+        late.append(
+            lambda b=b: add(acc, t_hi, t_lo, z_s, slice(b * block, (b + 1) * block), 2 * nkz)
+        )
+    late.pop()()
+
+
+def finish(sizes, acc, dacc, xtab, dens_ref, spec_ref):
     nx, ny, nz, nky, nkz = sizes
-    dens_ref[...] = dacc[:, :CZ] + dacc[:, CZ:] + dacc_lo[...]
+    dens_ref[...] = dacc[...]
     wide = max(nx, LANES)
     per = wide // nx
     for g in range(nky // per):
-
-        def take(r0):
-            s = slice(r0, r0 + wide)
-            v = acc[s, : 2 * nkz] + acc[s, 2 * nkz :] + acc_lo[s]
-            return v.T
-
-        re = take(g * wide)
-        im = take(nky * nx + g * wide)
-        c_re = re[:nkz] - im[nkz:]
-        c_im = re[nkz:] + im[:nkz]
-        both = jnp.concatenate([c_re, c_im], axis=0)
-        q = jnp.dot(both, xtab[...], precision=highest, preferred_element_type=f32)
-        spec_ref[0, :, g * wide : (g + 1) * wide] = q[:nkz, :wide] + q[nkz:, wide:]
-        spec_ref[1, :, g * wide : (g + 1) * wide] = q[nkz:, :wide] - q[:nkz, wide:]
+        re = acc[g * wide : (g + 1) * wide]
+        im = acc[nky * nx + g * wide : nky * nx + (g + 1) * wide]
+        both = jnp.concatenate([re[:, :nkz] - im[:, nkz:], re[:, nkz:] + im[:, :nkz]], axis=1)
+        q = jnp.dot(xtab[...], both, precision=highest, preferred_element_type=f32)
+        s = slice(g * wide, (g + 1) * wide)
+        spec_ref[0, s] = q[:wide, :nkz] + q[wide:, nkz:]
+        spec_ref[1, s] = q[:wide, nkz:] - q[wide:, :nkz]
 
 
 def scratches(sizes):
@@ -199,11 +207,9 @@
         pltpu.VMEM((CX * CY, k), bf16),
         pltpu.VMEM((4 * nkz, k), bf16),
         pltpu.VMEM((2 * CZ, k), bf16),
-        pltpu.VMEM((2 * nky, SPAN), f32),
-        pltpu.VMEM((2 * nkz, SPAN), f32),
-        pltpu.VMEM((m, 4 * nkz), f32),
+        pltpu.VMEM((2 * nky, 3 * SPAN), bf16),
+        pltpu.VMEM((2 * nkz, 3 * SPAN), bf16),
         pltpu.VMEM((m, 2 * nkz), f32),
-        pltpu.VMEM((CX * CY, 2 * CZ), f32),
         pltpu.VMEM((CX * CY, CZ), f32),
     ]
 
@@ -211,12 +217,12 @@
 def start_work(sizes, place, refs):
     nx, ny, nz, nky, nkz = sizes
     gx, gy, gz, kz0 = place
-    ytab, ztab, acc, acc_lo, dacc, dacc_lo = refs[-6:]
+    ytab, ztab, acc, dacc = refs[-4:]
     kyc = iota_f((nky, 1), 0) + (gx * nky).astype(f32)
     kzc = iota_f((nkz, 1), 0) + (kz0 * nkz).astype(f32)
     ytab[...] = span_table(kyc, ny)
     ztab[...] = span_table(kzc, nz)
-    for r in (acc, acc_lo, dacc, dacc_lo):
+    for r in (acc, dacc):
         r[...] = jnp.zeros_like(r)
 
 
@@ -226,14 +232,14 @@
 
 
 def unpack(blocks, prm):
-    owner = lax.broadcasted_iota(jnp.int32, (SPAN, LANES), 1) // (LANES // len(blocks))
-    for g in range(prm.shape[0] // SPAN):
+    owner = lax.broadcasted_iota(jnp.int32, (GROUP, LANES), 1) // (LANES // len(blocks))
+    for g in range(prm.shape[0] // GROUP):
         v = None
         for d, block in enumerate(blocks):
             shift = (d - g) % len(blocks) * (LANES // len(blocks))
             w = pltpu.roll(block, shift, 1) if shift else block
             v = w if v is None else jnp.where(owner == d, w, v)
-        prm[g * SPAN : (g + 1) * SPAN] = v
+        prm[g * GROUP : (g + 1) * GROUP] = v
 
 
 def kernel(sizes, counts, own_ref, xtab, dens_ref, spec_ref, prm, cols, *refs):
@@ -305,7 +311,7 @@
         return carry
 
     lax.fori_loop(0, n_col, step, 0)
-    finish(sizes, *refs[-4:], xtab, dens_ref, spec_ref)
+    finish(sizes, *refs[-2:], xtab, dens_ref, spec_ref)
     for r in range(1, n_gz):
         copy_z(r).wait_send()
 
@@ -323,7 +329,7 @@
     eye = np.eye(wide // nx)
     scale = 1.0 / math.sqrt(total)
     return np.concatenate(
-        [np.kron(eye, np.cos(angle)), np.kron(eye, np.sin(angle))], axis=1
+        [np.kron(eye, np.cos(angle)), np.kron(eye, np.sin(angle))], axis=0
     ).astype(np.float32) * np.float32(scale)
 
 
@@ -344,22 +350,22 @@
         [coefs, pair_cells.astype(f32), pair_offsets, rate[None], radius[None]], axis=0
     )
     pair_dev = prm.shape[1]
-    assert prm.shape[0] == 3 * SPAN and n_gz * pair_dev == LANES and n_gz >= 3
-    groups = [prm[g * SPAN : (g + 1) * SPAN] for g in range(3)]
-    groups.append(jnp.zeros((SPAN, LANES - 3 * pair_dev), f32))
+    assert prm.shape[0] == 3 * GROUP and n_gz * pair_dev == LANES and n_gz >= 3
+    groups = [prm[g * GROUP : (g + 1) * GROUP] for g in range(3)]
+    groups.append(jnp.zeros((GROUP, LANES - 3 * pair_dev), f32))
     own = jnp.concatenate(groups, axis=1)
     n_col = n_gx * n_gy
     dens, spec = pl.pallas_call(
         functools.partial(kernel, sizes, (n_gx, n_gy, n_gz)),
         out_shape=[
             jax.ShapeDtypeStruct((CX * CY, CZ), f32),
-            jax.ShapeDtypeStruct((2, nkz, nky * nx), f32),
+            jax.ShapeDtypeStruct((2, nky * nx, nkz), f32),
         ],
         in_specs=[pl.BlockSpec(memory_space=pltpu.VMEM)] * 2,
         out_specs=[pl.BlockSpec(memory_space=pltpu.VMEM)] * 2,
         scratch_shapes=[
-            pltpu.VMEM((3 * SPAN, LANES), f32),
-            pltpu.VMEM((n_col, n_gz, SPAN, LANES), f32),
+            pltpu.VMEM((3 * GROUP, LANES), f32),
+            pltpu.VMEM((n_col, n_gz, GROUP, LANES), f32),
             *scratches(sizes),
             pltpu.SemaphoreType.DMA((n_gz,)),
             pltpu.SemaphoreType.DMA((n_gz,)),
@@ -368,7 +374,7 @@
         ],
         compiler_params=pltpu.CompilerParams(collective_id=0, has_side_effects=True),
     )(own, jnp.asarray(x_table(nx, nx * ny * nz)))
-    return dens.reshape(CX, CY, CZ), spec.reshape(2, nkz, nky, nx)
+    return dens.reshape(CX, CY, CZ), spec.reshape(2, nky, nx, nkz).transpose(0, 3, 1, 2)
 
 
 def solution(mesh):

time: 40.1 us -> 38.5 us (0.960)
  Pallas kernels: 32.4 us -> 30 us
  local copies, waits for them, and re-layouts: 4.04 us -> 4.83 us
    unnamed x11 -> x10, local copies, waits for them, and re-layouts: 1.94 us -> 4.72 us
    pallas_call x1, Pallas kernels: 32.4 us -> 30 us  [shards(): pl.pallas_call(functools.partial(kernel, sizes, (n_gx, n_gy, n_gz)), out_...]
    pallas_call x1 -> x0, local copies, waits for them, and re-layouts: 1.98 us -> none  [shards(): pl.pallas_call(functools.partial(kernel, sizes, (n_gx, n_gy, n_gz)), out_...]
where the time goes in v3:
time: 38.5 us; the launch traced here: 38.2 us
  Pallas kernels  30 us (78%)
  local copies, waits for them, and re-layouts  4.83 us (13%)
  other arithmetic  1.49 us (4%)
  matrix products  1.15 us (3%)
  between operations  0.71 us (2%)
    pallas_call x1, Pallas kernels, shards(): pl.pallas_call(functools.partial(kernel, sizes, (n_gx, n_gy, n_gz)), out_...  30 us
    unnamed x10, local copies, waits for them, and re-layouts  4.72 us
    dot_general x1, matrix products, shards(): coefs = jnp.dot(basis_map.T, pair_blocks, precision=highest)  1.15 us
    reduce_sum x1, other arithmetic, shards(): rate = jnp.sum(exponents[:, None] * selector, axis=0) / (radius * radius)  0.8 us

profile of v3, /device:TPU:0, one launch (start us, length us, event | category | flops | bytes accessed | tf_op | source)
XLA Modules:
  0.0 38.2 jit_solution(12427217432350951463)
XLA Ops:
  0.6 0.0 copy-start
  0.6 0.0 copy-start.3
  0.7 0.8 %select_reduce_fusion = f32[32]{0:T(128)S(1)} fusion(f32[16]{0:T(128)} %param.14, s32[32]{0:T(128)} %param.12), kind=kLoop, calls=%fused_computation.1 | loop fusion | flops 1504 | bytes 320 | tf_op jit(solution)/shard_map/reduce_sum | solution.py:347
  1.5 0.0 copy-done.3
  1.5 0.0 copy-start.2
  1.5 0.1 pad.3.clone
  1.6 0.6 %copy-done.2 = s32[3,32]{1,0:T(4,128)S(1)} copy-done((s32[3,32]{1,0:T(4,128)S(1)}, s32[3,32]{1,0:T(4,128)}, u32[]{:S(2)}) %copy-start.2) | copy-done | bytes 408
  2.2 0.0 copy-done
  2.2 1.2 %fusion.2 = f32[64,32]{1,0:T(8,128)S(1)} fusion(f32[529,64]{0,1:T(8,128)S(1)} %copy-done, f32[529,32]{0,1:T(8,128)} %param.8), kind=kOutput, calls=%fused_computation.7 | convolution fusion | flops 13000704 | bytes 211328 | tf_op jit(solution)/shard_map/dot_general | solution.py:348
  3.4 0.0 copy-start.1
  3.4 0.7 %copy-done.1 = f32[3,32]{1,0:T(4,128)S(1)} copy-done((f32[3,32]{1,0:T(4,128)S(1)}, f32[3,32]{1,0:T(4,128)}, u32[]{:S(2)}) %copy-start.1) | copy-done | bytes 408
  4.1 0.7 %maximum_maximum_fusion.own_ref = f32[24,128]{1,0:T(8,128)} fusion(f32[24,32]{1,0:T(8,128)S(1)} %slice.14, f32[24,32]{1,0:T(8,128)S(1)} %get-tuple-element.7, f32[24,32]{1,0:T(8,128)S(1)} %get-tuple-element.6, f32[128]{0:T(128)S(1)} %pad.3.clone), kind=kLoop, calls=%fused_computation | loop fusion | flops 9216 | bytes 22016 | tf_op jit(solution)/shard_map/concatenate | solution.py:356
  4.7 30.0 %shard_map.95 = (f32[256,128]{1,0:T(8,128)}, f32[2,512,64]{2,1,0:T(8,128)}) custom-call(f32[24,128]{1,0:T(8,128)} %maximum_maximum_fusion.own_ref, f32[256,128]{1,0:T(8,128)} %constant.8.clone.xtab), custom_call_target="tpu_custom_call" | custom-call | tf_op jit(solution)/shard_map/pallas_call | solution.py:358
  34.8 1.6 %copy.26 = f32[8,32,128]{2,1,0:T(8,128)} copy(f32[8,32,128]{2,1,0:T(8,128)} %bitcast.11) | data formatting | bytes 262144
  36.3 1.9 %copy.27 = f32[2,64,16,32]{1,3,2,0:T(8,128)} copy(f32[2,64,16,32]{1,3,2,0:T(8,128)} %bitcast.10) | data formatting | bytes 524288
  (7 shorter events, 0.1 us)
Async XLA Ops:
  0.6 1.5 %copy-start = (f32[529,64]{0,1:T(8,128)S(1)}, f32[529,64]{0,1:T(8,128)}, u32[]{:S(2)}) copy-start(f32[529,64]{0,1:T(8,128)} %param.9) | copy-start | bytes 406276
  0.6 0.8 %copy-start.3 = (s32[32]{0:T(128)S(1)}, s32[32]{0:T(128)}, u32[]{:S(2)}) copy-start(s32[32]{0:T(128)} %param.13) | copy-start | bytes 388
  1.5 0.7 %copy-start.2 = (s32[3,32]{1,0:T(4,128)S(1)}, s32[3,32]{1,0:T(4,128)}, u32[]{:S(2)}) copy-start(s32[3,32]{1,0:T(4,128)} %param.10) | copy-start | bytes 1156
  3.4 0.7 %copy-start.1 = (f32[3,32]{1,0:T(4,128)S(1)}, f32[3,32]{1,0:T(4,128)}, u32[]{:S(2)}) copy-start(f32[3,32]{1,0:T(4,128)} %param.11) | copy-start | bytes 1156
